TPU v7x, 32 devices: a whole 2x2x4 slice. The times are simulated.
32 devices in a mesh: dp: 8 (over z, core), expert: 4 (over y, x).
Axes of the slice: x: 2, y: 2, z: 4, core: 2. Of those that a mesh axis runs over, the one named last changes fastest.
Arguments:
- attention_gradient: bfloat16 [8, 6144, 1024], P('dp', None, 'expert')
- attention_weight: float32 [6144, 1024], P('dp', 'expert'), may hold values from -6 to 6
- attention_mean: float32 [6144, 1024], P('dp', 'expert'), may hold values from -0.0012 to 0.0012
- attention_square: float32 [6144, 1024], P('dp', 'expert'), may hold values from 1e-09 to 1e-07
- expert_gradient: float32 [8, 4, 8, 6144], P('dp', 'expert')
- expert_weight: float32 [8, 4, 8, 6144], P('dp', 'expert'), may hold values from -6 to 6
- held_mean: float32 [8, 32, 6144], P('dp', 'expert'), may hold values from -0.0006 to 0.0006
- held_square: float32 [8, 32, 6144], P('dp', 'expert'), may hold values from 1e-10 to 1e-08
- live_block_count: int32 [4], replicated, may hold values from 1 to 8, as said below
- holder_table: int32 [4, 8], replicated, may hold values from 0 to 3, as said below
- slot_table: int32 [4, 8], replicated, may hold values from 0 to 7, as said below
- step_count: int32 [1], replicated, may hold values from 1 to 40
Outputs:
- updated_attention: float32 [6144, 1024], P('dp', 'expert')
- updated_means: float32 [6144, 1024], P('dp', 'expert')
- updated_squares: float32 [6144, 1024], P('dp', 'expert')
- updated_experts: float32 [8, 4, 8, 6144], P('dp', 'expert')
- expert_means: float32 [8, 4, 8, 6144], P('dp', 'expert')
- expert_squares: float32 [8, 4, 8, 6144], P('dp', 'expert')
Inputs may be any that keep to these rules, and one draw needn't show every extreme that they name: `live_block_count`: every expert has 1 to 8 live blocks and some expert has exactly 8. `holder_table`: no holder holds more than 2 live blocks of one expert, and some holder holds exactly 2 of one. `slot_table`: the blocks on one holder sit in distinct slots, and some holder has all 8 slots live.
All inputs are finite; a program needn't handle non-finite values.
Results may differ from a plain program's by a relative error of at most 0.0003.
Values sent between devices are 32-bit elements; how exact they have to be, the bound alone decides.
A program may use at most 64 MiB of HBM per device.

v0:
```python
import functools

import jax
import jax.numpy as jnp
from jax import lax
from jax.experimental import pallas as pl
from jax.experimental.pallas import tpu as pltpu
from jax.sharding import PartitionSpec as P

MESH = pl.DeviceIdType.MESH
CORES = 2
LAG = 1
LIMIT = 40 * 1024 * 1024

beta_first = 0.9
beta_second = 0.95
learn_rate = 0.1
decay_rate = 0.1
adam_epsilon = 1e-08
clip_norm = 1.0


def power(base, exponent):
    result = jnp.float32(1.0)
    value = base
    for bit in range(31):
        factor = value if value > 1e-37 else 0.0
        result = jnp.where((exponent >> bit) & 1 == 1, result * jnp.float32(factor), result)
        value = value * value
    return result


def adam_step(weight, mean, square, gradient, factor, first_scale, second_scale):
    scaled = factor * gradient
    mean_new = beta_first * mean + (1.0 - beta_first) * scaled
    square_new = beta_second * square + (1.0 - beta_second) * scaled * scaled
    mean_hat = mean_new * first_scale
    square_hat = square_new * second_scale
    weight_new = weight - learn_rate * (
        mean_hat / (jnp.sqrt(square_hat) + adam_epsilon) + decay_rate * weight
    )
    return weight_new, mean_new, square_new


def kernel(
    levels, experts, pieces, per_holder,
    grad_hbm, eg_hbm, ew_hbm, w_hbm, m_hbm, v_hbm, hm_hbm, hs_hbm, count_hbm, holder_hbm, slot_hbm, step_ref,
    sum_ref, own_mean, own_square, scale_ref, live_ref, eg, ew, w_in, m_in, v_in,
    grad, pair_out, local, recv, hm, hs,
    out_mean, out_square, in_mean, in_square, part, parts, count_ref, holder_ref, slot_ref,
    grad_sem, load_sem, pair_send, pair_recv, link_send, link_recv,
    mom_send, mom_recv, part_send, part_recv,
):
    dp = lax.axis_index("dp")
    me = lax.axis_index("expert")
    z = dp // CORES
    core = dp % CORES
    other = 1 - core
    partner = z * CORES + other
    upper = 2 * z >= levels
    maxb = holder_ref.shape[1]
    total_pieces = levels * pieces
    devices = levels * CORES * experts

    def level_of(j):
        return jnp.where(upper, j, levels - 1 - j)

    def grad_load(j):
        d = level_of(j)
        return pltpu.make_async_copy(grad_hbm.at[d], grad.at[d], grad_sem.at[j])

    for j in range(levels):
        grad_load(j).start()
    loads = [
        pltpu.make_async_copy(a, b, load_sem.at[i])
        for i, (a, b) in enumerate(
            (
                (count_hbm, count_ref), (holder_hbm, holder_ref), (slot_hbm, slot_ref),
                (hm_hbm, hm), (hs_hbm, hs), (eg_hbm, eg),
                (ew_hbm, ew), (w_hbm, w_in), (m_hbm, m_in), (v_hbm, v_in),
            )
        )
    ]
    barrier = pltpu.get_barrier_semaphore()
    pl.semaphore_signal(barrier, inc=1, device_id=(partner, me), device_id_type=MESH)
    for off in range(1, experts):
        pl.semaphore_signal(barrier, inc=1, device_id=(dp, lax.rem(me + off, experts)), device_id_type=MESH)

    @pl.when(z > 0)
    def _():
        pl.semaphore_signal(barrier, inc=1, device_id=(dp - CORES, me), device_id_type=MESH)

    @pl.when(z < levels - 1)
    def _():
        pl.semaphore_signal(barrier, inc=1, device_id=(dp + CORES, me), device_id_type=MESH)

    first = level_of(0)
    grad_load(0).wait()

    @pl.loop(0, pieces)
    def _(p):
        pair_out[first, p] = grad[first, other, p].astype(jnp.float32)

    near = jnp.where(z > 0, 1, 0) + jnp.where(z < levels - 1, 1, 0)
    pl.semaphore_wait(barrier, experts + near)

    def pair_copy(d, p):
        return pltpu.make_async_remote_copy(
            src_ref=pair_out.at[d, p], dst_ref=local.at[d, p],
            send_sem=pair_send.at[d * pieces + p], recv_sem=pair_recv.at[d * pieces + p],
            device_id=(partner, me), device_id_type=MESH,
        )

    def link_copy(way, d, p, src):
        return pltpu.make_async_remote_copy(
            src_ref=src, dst_ref=recv.at[way, d, p],
            send_sem=link_send.at[way, d * pieces + p], recv_sem=link_recv.at[way, d * pieces + p],
            device_id=(jnp.where(way == 0, dp + CORES, dp - CORES), me), device_id_type=MESH,
        )

    def give(j):
        grad_load(j).wait()
        d = level_of(j)

        @pl.loop(0, pieces)
        def _(p):
            pair_out[d, p] = grad[d, other, p].astype(jnp.float32)
            pair_copy(d, p).start()

    way_out = jnp.where(upper, 1, 0)
    at_end = (z == 0) | (z == levels - 1)

    def take(j):
        d = level_of(j)

        @pl.loop(0, pieces)
        def _(p):
            pair_copy(d, p).wait_recv()
            local[d, p] = local[d, p] + grad[d, core, p].astype(jnp.float32)

            @pl.when(at_end & (d != z))
            def _():
                link_copy(way_out, d, p, local.at[d, p]).start()

    @pl.loop(0, pieces)
    def _(p):
        pair_copy(first, p).start()

    for load in loads[:5]:
        load.start()

    @pl.loop(0, levels)
    def _(j):
        @pl.when(j + 1 < levels)
        def _():
            give(j + 1)

        take(j)

    for load in loads[5:]:
        load.start()
    for load in loads[:5]:
        load.wait()

    def moment_copy(which, src, dst, target, source):
        return pltpu.make_async_remote_copy(
            src_ref=src.at[target], dst_ref=dst.at[source],
            send_sem=mom_send.at[which, target], recv_sem=mom_recv.at[which, source],
            device_id=(dp, target), device_id_type=MESH,
        )

    def picks(owner):
        rank = jnp.int32(0)
        chosen = [jnp.int32(0)] * per_holder
        for b in range(maxb):
            mine = (holder_ref[owner, b] == me) & (b < count_ref[owner])
            for q in range(per_holder):
                chosen[q] = jnp.where(mine & (rank == q), slot_ref[owner, b], chosen[q])
            rank = rank + jnp.where(mine, 1, 0)
        return chosen

    for q, slot in enumerate(picks(me)):
        in_mean[me, pl.ds(q, 1), :] = hm[pl.ds(slot, 1), :]
        in_square[me, pl.ds(q, 1), :] = hs[pl.ds(slot, 1), :]

    @pl.loop(1, experts)
    def _(off):
        owner = lax.rem(me + off, experts)
        for q, slot in enumerate(picks(owner)):
            out_mean[owner, pl.ds(q, 1), :] = hm[pl.ds(slot, 1), :]
            out_square[owner, pl.ds(q, 1), :] = hs[pl.ds(slot, 1), :]
        moment_copy(0, out_mean, in_mean, owner, me).start()
        moment_copy(1, out_square, in_square, owner, me).start()

    def forward(way, k):
        j = k // pieces
        p = k % pieces
        d = jnp.where(way == 0, levels - 1 - j, j)
        ahead = jnp.where(way == 0, (d > z) & (z > 0), (d < z) & (z < levels - 1))

        @pl.when(ahead)
        def _():
            copy = link_copy(way, d, p, recv.at[way, d, p])
            copy.wait_recv()
            recv[way, d, p] = recv[way, d, p] + local[d, p]
            copy.start()

    @pl.loop(0, total_pieces + LAG)
    def _(s):
        @pl.when(s < total_pieces)
        def _():
            forward(way_out, s)

        @pl.when(s >= LAG)
        def _():
            forward(1 - way_out, s - LAG)

    @pl.loop(1, experts)
    def _(off):
        source = lax.rem(me + off, experts)
        moment_copy(0, out_mean, in_mean, source, source).wait()
        moment_copy(1, out_square, in_square, source, source).wait()

    owned = count_ref[me]
    for b in range(maxb):
        holder = holder_ref[me, b]
        rank = jnp.int32(0)
        for earlier in range(b):
            rank = rank + jnp.where((holder_ref[me, earlier] == holder) & (earlier < owned), 1, 0)
        rank = jnp.minimum(rank, per_holder - 1)
        own_mean[pl.ds(b, 1), :] = in_mean[holder, pl.ds(rank, 1), :]
        own_square[pl.ds(b, 1), :] = in_square[holder, pl.ds(rank, 1), :]
    for load in loads[5:]:
        load.wait()
    width = eg.shape[1]
    live = lax.broadcasted_iota(jnp.int32, (maxb, 128), 0) < owned
    acc = jnp.zeros((maxb, 128), jnp.float32)
    for i in range(width // 128):
        g = eg[:, pl.ds(i * 128, 128)]
        acc = acc + jnp.where(live, g * g, 0.0)
    row = jnp.sum(acc, axis=0, keepdims=True)
    live_ref[...] = jnp.where(live, 1.0, 0.0)
    step = step_ref[0]
    one = jnp.ones((1, 128), jnp.float32)
    scale_ref[1:2] = 1.0 / (one * (1.0 - power(beta_first, step)))
    scale_ref[2:3] = 1.0 / (one * (1.0 - power(beta_second, step)))

    def finish(p, row):
        sum_ref[p] = local[z, p]

        @pl.when(z < levels - 1)
        def _():
            link_copy(1, z, p, recv.at[1, z, p]).wait_recv()

            @pl.when(z > 0)
            def _():
                link_copy(0, z, p, recv.at[0, z, p]).wait_recv()
                sum_ref[p] = local[z, p] + (recv[0, z, p] + recv[1, z, p])

            @pl.when(z == 0)
            def _():
                sum_ref[p] = local[z, p] + recv[1, z, p]

        @pl.when((z == levels - 1) & (z > 0))
        def _():
            link_copy(0, z, p, recv.at[0, z, p]).wait_recv()
            sum_ref[p] = local[z, p] + recv[0, z, p]

        g = sum_ref[p]
        col = jnp.sum(g * g, axis=0, keepdims=True)
        for i in range(g.shape[1] // 128):
            row = row + col[:, i * 128:(i + 1) * 128]
        return row

    row = lax.fori_loop(0, pieces, finish, row)

    index = dp * experts + me
    part[...] = row
    parts[index] = row

    def part_copy(off):
        target = lax.rem(index + off, devices)
        return pltpu.make_async_remote_copy(
            src_ref=part, dst_ref=parts.at[index],
            send_sem=part_send.at[off], recv_sem=part_recv,
            device_id=(target // experts, lax.rem(target, experts)), device_id_type=MESH,
        )

    @pl.loop(1, devices)
    def _(off):
        part_copy(off).start()

    @pl.loop(0, total_pieces)
    def _(k):
        d = k // pieces
        p = k % pieces
        pair_copy(d, p).wait_send()

        @pl.when(d > z)
        def _():
            link_copy(0, d, p, local.at[d, p]).wait_send()

        @pl.when(d < z)
        def _():
            link_copy(1, d, p, local.at[d, p]).wait_send()

    others = parts.at[pl.ds(0, devices - 1)]
    pltpu.make_async_copy(others, others, part_recv).wait()
    total = jnp.sum(jnp.sum(parts[...], axis=0), axis=1, keepdims=True)
    scale_ref[0:1] = jnp.broadcast_to(jnp.minimum(1.0, clip_norm / (jnp.sqrt(total) + 1e-06)), (1, 128))

    @pl.loop(1, devices)
    def _(off):
        part_copy(off).wait_send()


def update(
    w_in, m_in, v_in, sums, eg, ew, own_mean, own_square, scale_ref, live_ref,
    ow_hbm, om_hbm, ov_hbm, oew_hbm, oem_hbm, oes_hbm,
    ow, om, ov, oew, oem, oes, sem, expert_sem,
):
    factor = scale_ref[0:1, 0:1]
    first_scale = scale_ref[1:2, 0:1]
    second_scale = scale_ref[2:3, 0:1]
    pieces = w_in.shape[0]
    triples = ((ow, ow_hbm), (om, om_hbm), (ov, ov_hbm))

    def put(i, p):
        src, dst = triples[i]
        return pltpu.make_async_copy(src.at[p], dst.at[p], sem.at[i, p])

    @pl.loop(0, pieces)
    def _(p):
        w_new, m_new, v_new = adam_step(
            w_in[p], m_in[p], v_in[p], sums[p], factor, first_scale, second_scale
        )
        ow[p] = w_new
        om[p] = m_new
        ov[p] = v_new
        for i in range(3):
            put(i, p).start()

    maxb, width = eg.shape
    live = live_ref[...] > 0.5
    for i in range(width // 128):
        cols = pl.ds(i * 128, 128)
        w_old = ew[:, cols]
        w_new, m_new, v_new = adam_step(
            w_old, jnp.where(live, own_mean[:, cols], 0.0), jnp.where(live, own_square[:, cols], 0.0),
            eg[:, cols], factor, first_scale, second_scale,
        )
        oew[:, cols] = jnp.where(live, w_new, w_old)
        oem[:, cols] = jnp.where(live, m_new, 0.0)
        oes[:, cols] = jnp.where(live, v_new, 0.0)
    rest = [
        pltpu.make_async_copy(a, b, expert_sem.at[i])
        for i, (a, b) in enumerate(((oew, oew_hbm), (oem, oem_hbm), (oes, oes_hbm)))
    ]
    for copy in rest:
        copy.start()

    @pl.loop(0, pieces)
    def _(p):
        for i in range(3):
            put(i, p).wait()

    for copy in rest:
        copy.wait()


def piece_rows(rows):
    for size in range(192, 0, -16):
        if rows % size == 0:
            return size
    return rows


def make_body(mesh):
    n_dp = mesh.shape["dp"]
    experts = mesh.shape["expert"]
    levels = n_dp // CORES

    def body(ag, aw, am, av, eg, ew, hm, hs, count, holder, slot, step):
        depth, cols = ag.shape[1], ag.shape[2]
        rows = depth // n_dp
        size = piece_rows(rows)
        pieces = rows // size
        maxb, width = eg.shape[2], eg.shape[3]
        slots = hm.shape[1]
        per_holder = max(1, maxb // experts)
        f32 = jnp.float32
        own = (pieces, size, cols)
        k = levels * pieces
        dma = pltpu.SemaphoreType.DMA
        hbm = pl.BlockSpec(memory_space=pltpu.HBM)
        vmem = pl.BlockSpec(memory_space=pltpu.VMEM)
        blocks = (maxb, width)
        shape = jax.ShapeDtypeStruct
        moved = (experts, per_holder, width)
        sums, own_mean, own_square, scales, live, eg_in, ew_in, w_in, m_in, v_in = pl.pallas_call(
            functools.partial(kernel, levels, experts, pieces, per_holder),
            out_shape=[pltpu.VMEM(s, f32) for s in (own, blocks, blocks, (3, 128), (maxb, 128), blocks, blocks, own, own, own)],
            in_specs=[hbm] * 11 + [pl.BlockSpec(memory_space=pltpu.SMEM)],
            out_specs=[vmem] * 10,
            scratch_shapes=[
                pltpu.VMEM((levels, CORES, pieces, size, cols), ag.dtype),
                pltpu.VMEM((levels, pieces, size, cols), f32),
                pltpu.VMEM((levels, pieces, size, cols), f32),
                pltpu.VMEM((2, levels, pieces, size, cols), f32),
                pltpu.VMEM((slots, width), f32), pltpu.VMEM((slots, width), f32),
                pltpu.VMEM(moved, f32), pltpu.VMEM(moved, f32),
                pltpu.VMEM(moved, f32), pltpu.VMEM(moved, f32),
                pltpu.VMEM((1, 128), f32), pltpu.VMEM((n_dp * experts, 1, 128), f32),
                pltpu.SMEM(count.shape, jnp.int32), pltpu.SMEM(holder.shape, jnp.int32),
                pltpu.SMEM(slot.shape, jnp.int32),
                dma((levels,)), dma((10,)), dma((k,)), dma((k,)), dma((2, k)), dma((2, k)),
                dma((2, experts)), dma((2, experts)), dma((n_dp * experts,)), dma(()),
            ],
            compiler_params=pltpu.CompilerParams(
                collective_id=0, has_side_effects=True, vmem_limit_bytes=LIMIT
            ),
        )(
            *(pltpu.with_memory_space_constraint(x, pltpu.HBM) for x in (
                ag.reshape(levels, CORES, pieces, size, cols), eg[0, 0], ew[0, 0],
                aw.reshape(own), am.reshape(own), av.reshape(own), hm[0], hs[0],
                count, holder, slot,
            )),
            step,
        )
        outs = pl.pallas_call(
            update,
            out_shape=[shape(own, f32)] * 3 + [shape(blocks, f32)] * 3,
            in_specs=[vmem] * 10,
            out_specs=[hbm] * 6,
            scratch_shapes=[pltpu.VMEM(own, f32)] * 3 + [pltpu.VMEM(blocks, f32)] * 3 + [dma((3, pieces)), dma((3,))],
            compiler_params=pltpu.CompilerParams(vmem_limit_bytes=16 * 1024 * 1024),
        )(
            w_in, m_in, v_in, sums, eg_in, ew_in, own_mean, own_square, scales, live,
        )
        return tuple(o.reshape(rows, cols) for o in outs[:3]) + tuple(o[None, None] for o in outs[3:])

    return body


def solution(mesh):
    matrix = P("dp", "expert")
    blocks = P("dp", "expert", None, None)
    held = P("dp", "expert", None)
    return jax.shard_map(
        make_body(mesh),
        mesh=mesh,
        in_specs=(P("dp", None, "expert"), matrix, matrix, matrix, blocks, blocks, held, held, P(), P(), P(), P()),
        out_specs=(matrix, matrix, matrix, blocks, blocks, blocks),
        check_vma=False,
    )
```

profile of v0, /device:TPU:0, one launch (start us, length us, event | category | flops | bytes accessed | tf_op | source)
XLA Modules:
  0.0 68.7 jit_solution(2582337378435924622)
XLA Ops:
  1.3 65.2 %shard_map.163 = (f32[4,192,256]{2,1,0:T(8,128)S(1)}, f32[8,6144]{1,0:T(8,128)S(1)}, f32[8,6144]{1,0:T(8,128)S(1)}, f32[3,128]{1,0:T(4,128)S(1)}, f32[8,128]{1,0...) custom-call(bf16[4,2,4,192,256]{4,3,2,1,0:T(8,128)(2,1)} %bitcast.14, ...), custom_call_target="tpu_custom_call" | custom-call | tf_op jit(solution)/shard_map/pallas_call | solution.py:400
  66.5 2.2 %shard_map.164 = (f32[4,192,256]{2,1,0:T(8,128)}, f32[4,192,256]{2,1,0:T(8,128)}, f32[4,192,256]{2,1,0:T(8,128)}, f32[8,6144]{1,0:T(8,128)}, f32[8,6144]{1,0:T(8,128)}, /*index=5*/f32[8,6144]{1,0:T(8,128)}) custom-call(f32[4,192,256]{2,1,0:T(8,128)S(1)} %get-tuple-element.22.w_in, f32[4,192,256]{2,1,0:T(8,128)S(1)} %get-tuple-element.23.m_in, ...), custom_call_target="tpu_custom_call" | custom-call | tf_op jit(solution)/shard_map/pallas_call | solution.py:430
where the time goes:
time: 68.9 us; the launch traced here: 68.7 us
  Pallas kernels  67.4 us (98%)
  between operations  1.29 us (2%)
    pallas_call x1, Pallas kernels, body(): pl.pallas_call(functools.partial(kernel, levels, experts, pieces, per_hol...  65.2 us
    pallas_call x1, Pallas kernels, body(): pl.pallas_call(update, out_shape=[shape(own, f32)] * 3 + [shape(blocks, f...  2.17 us

commit v1 on v0

v1 whole, which is shorter than its diff:
```python
import functools

import jax
import jax.numpy as jnp
from jax import lax
from jax.experimental import pallas as pl
from jax.experimental.pallas import tpu as pltpu
from jax.sharding import PartitionSpec as P

MESH = pl.DeviceIdType.MESH
CORES = 2
LIMIT = 40 * 1024 * 1024

beta_first = 0.9
beta_second = 0.95
learn_rate = 0.1
decay_rate = 0.1
adam_epsilon = 1e-08
clip_norm = 1.0


def power(base, exponent):
    result = jnp.float32(1.0)
    value = base
    for bit in range(31):
        factor = value if value > 1e-37 else 0.0
        result = jnp.where((exponent >> bit) & 1 == 1, result * jnp.float32(factor), result)
        value = value * value
    return result


def far_first(size):
    return sorted(range(size), key=lambda k: (-min(k, size - k), k))


def kernel(
    levels, experts, per_holder, cuts,
    grad_hbm, eg_hbm, ew_hbm, w_hbm, m_hbm, v_hbm, hm_hbm, hs_hbm, count_hbm, holder_hbm, slot_hbm, step_hbm,
    sum_ref, wmv, blocks, scale_ref,
    grad, pair_out, local, recv, held, mom_out, mom_in, part, parts,
    count_ref, holder_ref, slot_ref, step_ref,
    grad_sem, load_sem, pair_send, pair_recv, link_send, link_recv,
    mom_send, mom_recv, part_send, part_recv,
):
    dp = lax.axis_index("dp")
    me = lax.axis_index("expert")
    z = dp // CORES
    core = dp % CORES
    other = 1 - core
    partner = z * CORES + other
    upper = 2 * z >= levels
    maxb = holder_ref.shape[1]
    rows = sum_ref.shape[0]
    steps = len(cuts)
    devices = levels * CORES * experts
    spans = [pl.ds(start, size) for start, size in cuts]

    def level_of(j):
        return jnp.where(upper, j, levels - 1 - j)

    first = level_of(0)
    head = cuts[0][1]

    def load_level(j):
        d = level_of(j)
        return pltpu.make_async_copy(grad_hbm.at[d], grad.at[d], grad_sem.at[j])

    def load_first(i, start, size):
        span = pl.ds(start, size)
        return pltpu.make_async_copy(grad_hbm.at[first, :, span], grad.at[first, :, span], grad_sem.at[i])

    opening = [load_first(0, 0, head)]
    if rows > head:
        opening.append(load_first(levels, head, rows - head))
    opening[0].start()

    barrier = pltpu.get_barrier_semaphore()
    pl.semaphore_signal(barrier, inc=1, device_id=(partner, me), device_id_type=MESH)

    @pl.when(z > 0)
    def _():
        pl.semaphore_signal(barrier, inc=1, device_id=(dp - CORES, me), device_id_type=MESH)

    @pl.when(z < levels - 1)
    def _():
        pl.semaphore_signal(barrier, inc=1, device_id=(dp + CORES, me), device_id_type=MESH)

    for off in range(1, experts):
        pl.semaphore_signal(barrier, inc=1, device_id=(dp, lax.rem(me + off, experts)), device_id_type=MESH)

    for load in opening[1:]:
        load.start()
    for j in range(1, levels):
        load_level(j).start()

    def pair_copy(d, span, sem):
        return pltpu.make_async_remote_copy(
            src_ref=pair_out.at[d, span], dst_ref=local.at[d, span],
            send_sem=pair_send, recv_sem=pair_recv.at[sem],
            device_id=(partner, me), device_id_type=MESH,
        )

    def link_copy(way, d, p, src):
        slot = d + 1 - way
        return pltpu.make_async_remote_copy(
            src_ref=src, dst_ref=recv.at[slot, spans[p]],
            send_sem=link_send, recv_sem=link_recv.at[slot, p],
            device_id=(jnp.where(way == 0, dp + CORES, dp - CORES), me), device_id_type=MESH,
        )

    way_out = jnp.where(upper, 1, 0)
    at_end = (z == 0) | (z == levels - 1)

    opening[0].wait()
    pair_out[first, spans[0]] = grad[first, other, spans[0]].astype(jnp.float32)
    near = jnp.where(z > 0, 1, 0) + jnp.where(z < levels - 1, 1, 0)
    pl.semaphore_wait(barrier, experts + near)
    pair_copy(first, spans[0], 0).start()
    for load in opening[1:]:
        load.wait()
    for p in range(1, steps):
        pair_out[first, spans[p]] = grad[first, other, spans[p]].astype(jnp.float32)
        pair_copy(first, spans[p], p).start()

    for p in range(steps):
        pair_copy(first, spans[p], p).wait_recv()
        local[first, spans[p]] = local[first, spans[p]] + grad[first, core, spans[p]].astype(jnp.float32)

        @pl.when(at_end & (first != z))
        def _():
            link_copy(way_out, first, p, local.at[first, spans[p]]).start()

    whole = pl.ds(0, rows)

    def give(j):
        load_level(j).wait()
        d = level_of(j)
        pair_out[d] = grad[d, other].astype(jnp.float32)
        pair_copy(d, whole, steps + j - 1).start()

    def take(j):
        d = level_of(j)
        pair_copy(d, whole, steps + j - 1).wait_recv()
        local[d] = local[d] + grad[d, core].astype(jnp.float32)

        @pl.when(at_end & (j < levels - 2))
        def _():
            for p in range(steps):
                link_copy(way_out, d, p, local.at[d, spans[p]]).start()

        @pl.when(at_end & (j == levels - 2))
        def _():
            for p in reversed(range(steps)):
                link_copy(way_out, d, p, local.at[d, spans[p]]).start()

    ints = [
        pltpu.make_async_copy(a, b, load_sem.at[i])
        for i, (a, b) in enumerate(((count_hbm, count_ref), (holder_hbm, holder_ref), (slot_hbm, slot_ref), (step_hbm, step_ref)))
    ]
    for load in ints:
        load.start()
    for i, source in enumerate((hm_hbm, hs_hbm)):
        pltpu.make_async_copy(source, held.at[i], load_sem.at[4]).start()

    if levels > 1:
        give(1)

    @pl.loop(1, levels)
    def _(j):
        @pl.when(j + 1 < levels)
        def _():
            give(j + 1)

        take(j)

    for i, source in enumerate((w_hbm, m_hbm, v_hbm)):
        pltpu.make_async_copy(source, wmv.at[i], load_sem.at[5]).start()
    for i, source in enumerate((eg_hbm, ew_hbm)):
        pltpu.make_async_copy(source, blocks.at[i], load_sem.at[6]).start()
    for load in ints:
        load.wait()
    pltpu.make_async_copy(held, held, load_sem.at[4]).wait()

    def moment_copy(target, source):
        return pltpu.make_async_remote_copy(
            src_ref=mom_out.at[target], dst_ref=mom_in.at[source],
            send_sem=mom_send, recv_sem=mom_recv,
            device_id=(dp, target), device_id_type=MESH,
        )

    def picks(owner):
        rank = jnp.int32(0)
        chosen = [jnp.int32(0)] * per_holder
        for b in range(maxb):
            mine = (holder_ref[owner, b] == me) & (b < count_ref[owner])
            for q in range(per_holder):
                chosen[q] = jnp.where(mine & (rank == q), slot_ref[owner, b], chosen[q])
            rank = rank + jnp.where(mine, 1, 0)
        return chosen

    for q, slot in enumerate(picks(me)):
        for i in range(2):
            mom_in[me, i, pl.ds(q, 1), :] = held[i, pl.ds(slot, 1), :]

    @pl.loop(1, experts)
    def _(off):
        owner = lax.rem(me + off, experts)
        for q, slot in enumerate(picks(owner)):
            for i in range(2):
                mom_out[owner, i, pl.ds(q, 1), :] = held[i, pl.ds(slot, 1), :]
        moment_copy(owner, me).start()

    def forward(way, j, p):
        d = jnp.where(way == 0, levels - 1 - j, j)
        ahead = jnp.where(way == 0, (d > z) & (z > 0), (d < z) & (z < levels - 1))
        slot = d + 1 - way

        @pl.when(ahead)
        def _():
            block = recv.at[slot, spans[p]]
            copy = link_copy(way, d, p, block)
            copy.wait_recv()
            recv[slot, spans[p]] = recv[slot, spans[p]] + local[d, spans[p]]
            copy.start()

    @pl.loop(0, levels)
    def _(j):
        for p in range(steps):
            forward(way_out, j, p)
            if p:
                forward(1 - way_out, j, p - 1)
            else:
                @pl.when(j > 0)
                def _():
                    forward(1 - way_out, j - 1, steps - 1)

    forward(1 - way_out, levels - 1, steps - 1)

    if experts > 1:
        others = mom_in.at[pl.ds(0, experts - 1)]
        pltpu.make_async_copy(others, others, mom_recv).wait()
        others = mom_out.at[pl.ds(0, experts - 1)]
        pltpu.make_async_copy(others, others, mom_send).wait()

    owned = count_ref[me]
    for b in range(maxb):
        holder = holder_ref[me, b]
        rank = jnp.int32(0)
        for earlier in range(b):
            rank = rank + jnp.where((holder_ref[me, earlier] == holder) & (earlier < owned), 1, 0)
        rank = jnp.minimum(rank, per_holder - 1)
        for i in range(2):
            blocks[2 + i, pl.ds(b, 1), :] = mom_in[holder, i, pl.ds(rank, 1), :]
    taken = blocks.at[pl.ds(0, 2)]
    pltpu.make_async_copy(taken, taken, load_sem.at[6]).wait()
    width = blocks.shape[2]
    live = lax.broadcasted_iota(jnp.int32, (maxb, 128), 0) < owned
    acc = jnp.zeros((maxb, 128), jnp.float32)
    for i in range(width // 128):
        span = pl.ds(i * 128, 128)
        g = jnp.where(live, blocks[0, :, span], 0.0)
        w = blocks[1, :, span]
        blocks[0, :, span] = g
        blocks[1, :, span] = jnp.where(live, (1.0 - learn_rate * decay_rate) * w, w)
        blocks[2, :, span] = jnp.where(live, beta_first * blocks[2, :, span], 0.0)
        blocks[3, :, span] = jnp.where(live, beta_second * blocks[3, :, span], 0.0)
        acc = acc + g * g
    row = jnp.sum(acc, axis=0, keepdims=True)
    pltpu.make_async_copy(wmv, wmv, load_sem.at[5]).wait()
    for i, scale in enumerate((1.0 - learn_rate * decay_rate, beta_first, beta_second)):
        wmv[i] = wmv[i] * scale
    step = step_ref[0]
    one = jnp.ones((1, 128), jnp.float32)
    first_left = one * (1.0 - power(beta_first, step))
    second_root = jnp.sqrt(one * (1.0 - power(beta_second, step)))
    scale_ref[2:3] = learn_rate * second_root / first_left
    scale_ref[3:4] = adam_epsilon * second_root

    early = 1 - way_out
    inner = jnp.where(upper, z > 0, z < levels - 1)
    outer = jnp.where(upper, z < levels - 1, z > 0)
    for p in range(steps):
        @pl.when(inner)
        def _():
            link_copy(early, z, p, recv.at[z + 1 - early, spans[p]]).wait_recv()
            sum_ref[spans[p]] = local[z, spans[p]] + recv[z + 1 - early, spans[p]]

        @pl.when(jnp.logical_not(inner))
        def _():
            sum_ref[spans[p]] = local[z, spans[p]]

    for p in reversed(range(steps)):
        @pl.when(outer)
        def _():
            link_copy(way_out, z, p, recv.at[z + 1 - way_out, spans[p]]).wait_recv()
            sum_ref[spans[p]] = sum_ref[spans[p]] + recv[z + 1 - way_out, spans[p]]

        g = sum_ref[spans[p]]
        col = jnp.sum(g * g, axis=0, keepdims=True)
        for i in range(g.shape[1] // 128):
            row = row + col[:, i * 128:(i + 1) * 128]

    index = dp * experts + me
    part[...] = row
    parts[index] = row

    def part_copy(target_dp, target_me):
        return pltpu.make_async_remote_copy(
            src_ref=part, dst_ref=parts.at[index],
            send_sem=part_send, recv_sem=part_recv,
            device_id=(target_dp, target_me), device_id_type=MESH,
        )

    if devices <= 64:
        for far in far_first(levels):
            side = lax.rem(z + far, levels) * CORES
            for off in far_first(experts):
                target = lax.rem(me + off, experts)
                for swap in range(CORES):
                    if far or off or swap:
                        part_copy(side + lax.rem(core + swap, CORES), target).start()
    else:
        @pl.loop(1, devices)
        def _(off):
            target = lax.rem(index + off, devices)
            part_copy(target // experts, lax.rem(target, experts)).start()

    pltpu.make_async_copy(pair_out, pair_out, pair_send).wait()
    if levels > 1:
        sent = local.at[pl.ds(0, levels - 1)]
        pltpu.make_async_copy(sent, sent, link_send).wait()
    others = parts.at[pl.ds(0, devices - 1)]
    pltpu.make_async_copy(others, others, part_send).wait()
    pltpu.make_async_copy(others, others, part_recv).wait()
    total = jnp.sum(jnp.sum(parts[...], axis=0), axis=1, keepdims=True)
    factor = jnp.broadcast_to(jnp.minimum(1.0, clip_norm / (jnp.sqrt(total) + 1e-06)), (1, 128))
    scale_ref[0:1] = (1.0 - beta_first) * factor
    scale_ref[1:2] = (1.0 - beta_second) ** 0.5 * factor


def update(
    wmv, sums, blocks, scale_ref,
    ow_hbm, om_hbm, ov_hbm, oew_hbm, oem_hbm, oes_hbm,
    out, block_out, sem, block_sem,
):
    first_factor = scale_ref[0:1, 0:1]
    second_factor = scale_ref[1:2, 0:1]
    rate = scale_ref[2:3, 0:1]
    epsilon = scale_ref[3:4, 0:1]
    rows = sums.shape[0]
    size = chunk_rows(rows)

    @pl.loop(0, rows // size)
    def _(c):
        span = pl.ds(pl.multiple_of(c * size, size), size)
        g = sums[span]
        m = wmv[1, span] + first_factor * g
        s = second_factor * g
        v = wmv[2, span] + s * s
        out[1, span] = m
        out[2, span] = v
        out[0, span] = wmv[0, span] - rate * m / (v * lax.rsqrt(v) + epsilon)
        for i, dst in enumerate((ow_hbm, om_hbm, ov_hbm)):
            pltpu.make_async_copy(out.at[i, span], dst.at[span], sem).start()

    width = blocks.shape[2]
    for i in range(width // 128):
        cols = pl.ds(i * 128, 128)
        g = blocks[0, :, cols]
        m = blocks[2, :, cols] + first_factor * g
        s = second_factor * g
        v = blocks[3, :, cols] + s * s
        block_out[1, :, cols] = m
        block_out[2, :, cols] = v
        block_out[0, :, cols] = blocks[1, :, cols] - rate * m / (jnp.sqrt(v) + epsilon)
    for i, dst in enumerate((oew_hbm, oem_hbm, oes_hbm)):
        pltpu.make_async_copy(block_out.at[i], dst, block_sem).start()
    pltpu.make_async_copy(out, out, sem).wait()
    pltpu.make_async_copy(block_out, block_out, block_sem).wait()


def chunk_rows(rows):
    for size in range(96, 0, -8):
        if rows % size == 0:
            return size
    return rows


def cut_rows(rows):
    if rows % 16:
        return ((0, rows),)
    head = max(16, rows // 12 // 16 * 16)
    half = (rows - head) // 2 // 16 * 16
    sizes = [size for size in (head, half, rows - head - half) if size > 0]
    starts = [sum(sizes[:i]) for i in range(len(sizes))]
    return tuple(zip(starts, sizes))


def make_body(mesh):
    n_dp = mesh.shape["dp"]
    experts = mesh.shape["expert"]
    levels = n_dp // CORES

    def body(ag, aw, am, av, eg, ew, hm, hs, count, holder, slot, step):
        depth, cols = ag.shape[1], ag.shape[2]
        rows = depth // n_dp
        cuts = cut_rows(rows)
        maxb, width = eg.shape[2], eg.shape[3]
        slots = hm.shape[1]
        per_holder = max(1, maxb // experts)
        f32 = jnp.float32
        dma = pltpu.SemaphoreType.DMA
        hbm = pl.BlockSpec(memory_space=pltpu.HBM)
        vmem = pl.BlockSpec(memory_space=pltpu.VMEM)
        shape = jax.ShapeDtypeStruct
        moved = (experts, 2, per_holder, width)
        sums, wmv, blocks, scales = pl.pallas_call(
            functools.partial(kernel, levels, experts, per_holder, cuts),
            out_shape=[pltpu.VMEM(s, f32) for s in ((rows, cols), (3, rows, cols), (4, maxb, width), (4, 128))],
            in_specs=[hbm] * 12,
            out_specs=[vmem] * 4,
            scratch_shapes=[
                pltpu.VMEM((levels, CORES, rows, cols), ag.dtype),
                pltpu.VMEM((levels, rows, cols), f32),
                pltpu.VMEM((levels, rows, cols), f32),
                pltpu.VMEM((levels + 1, rows, cols), f32),
                pltpu.VMEM((2, slots, width), f32),
                pltpu.VMEM(moved, f32), pltpu.VMEM(moved, f32),
                pltpu.VMEM((1, 128), f32), pltpu.VMEM((n_dp * experts, 1, 128), f32),
                pltpu.SMEM(count.shape, jnp.int32), pltpu.SMEM(holder.shape, jnp.int32),
                pltpu.SMEM(slot.shape, jnp.int32), pltpu.SMEM(step.shape, jnp.int32),
                dma((levels + 1,)), dma((7,)), dma(()), dma((len(cuts) + levels - 1,)),
                dma(()), dma((levels + 1, len(cuts))),
                dma(()), dma(()), dma(()), dma(()),
            ],
            compiler_params=pltpu.CompilerParams(
                collective_id=0, has_side_effects=True, vmem_limit_bytes=LIMIT
            ),
        )(
            *(pltpu.with_memory_space_constraint(x, pltpu.HBM) for x in (
                ag.reshape(levels, CORES, rows, cols), eg[0, 0], ew[0, 0],
                aw, am, av, hm[0], hs[0], count, holder, slot,
            )),
            step,
        )
        outs = pl.pallas_call(
            update,
            out_shape=[shape((rows, cols), f32)] * 3 + [shape((maxb, width), f32)] * 3,
            in_specs=[vmem] * 4,
            out_specs=[hbm] * 6,
            scratch_shapes=[pltpu.VMEM((3, rows, cols), f32), pltpu.VMEM((3, maxb, width), f32), dma(()), dma(())],
            compiler_params=pltpu.CompilerParams(vmem_limit_bytes=16 * 1024 * 1024),
        )(wmv, sums, blocks, scales)
        return tuple(outs[:3]) + tuple(o[None, None] for o in outs[3:])

    return body


def solution(mesh):
    matrix = P("dp", "expert")
    blocks = P("dp", "expert", None, None)
    held = P("dp", "expert", None)
    return jax.shard_map(
        make_body(mesh),
        mesh=mesh,
        in_specs=(P("dp", None, "expert"), matrix, matrix, matrix, blocks, blocks, held, held, P(), P(), P(), P()),
        out_specs=(matrix, matrix, matrix, blocks, blocks, blocks),
        check_vma=False,
    )
```

time: 68.9 us -> 66.3 us (0.962)
  Pallas kernels: 67.4 us -> 64.8 us
    pallas_call x2, Pallas kernels: 67.4 us -> 64.8 us  [the longest x1 63.1 us: body(): pl.pallas_call(functools.partial(kernel, levels, experts, per_holder, cut...]
where the time goes in v1:
time: 66.3 us; the launch traced here: 66.1 us
  Pallas kernels  64.8 us (98%)
  between operations  1.29 us (2%)
    pallas_call x1, Pallas kernels, body(): pl.pallas_call(functools.partial(kernel, levels, experts, per_holder, cut...  63.1 us
    pallas_call x1, Pallas kernels, body(): pl.pallas_call(update, out_shape=[shape((rows, cols), f32)] * 3 + [shape(...  1.68 us

profile of v1, /device:TPU:0, one launch (start us, length us, event | category | flops | bytes accessed | tf_op | source)
XLA Modules:
  0.0 66.1 jit_solution(14017897050094291800)
XLA Ops:
  1.3 63.1 %shard_map.163 = (f32[768,256]{1,0:T(8,128)S(1)}, f32[3,768,256]{2,1,0:T(8,128)S(1)}, f32[4,8,6144]{2,1,0:T(8,128)S(1)}, f32[4,128]{1,0:T(4,128)S(1)}) custom-call(bf16[4,2,768,256]{3,2,1,0:T(8,128)(2,1)} %bitcast.8, f32[8,6144]{1,0:T(8,128)} %bitcast.9, f32[8,6144]{1,0:T(8,128)} %bitcast.10, f32[768,256]{1,0:T(8,128)} %w_hbm.1, f32[768,256]{1,0:T(8,128)} %m_hbm.1, ...), custom_call_target="tpu_custom_call" | custom-call | tf_op jit(solution)/shard_map/pallas_call | solution.py:417
  64.4 1.7 %shard_map.164 = (f32[768,256]{1,0:T(8,128)}, f32[768,256]{1,0:T(8,128)}, f32[768,256]{1,0:T(8,128)}, f32[8,6144]{1,0:T(8,128)}, f32[8,6144]{1,0:T(8,128)}, /*index=5*/f32[8,6144]{1,0:T(8,128)}) custom-call(f32[3,768,256]{2,1,0:T(8,128)S(1)} %get-tuple-element.16.wmv, f32[768,256]{1,0:T(8,128)S(1)} %get-tuple-element.17.sums, ...), custom_call_target="tpu_custom_call" | custom-call | tf_op jit(solution)/shard_map/pallas_call | solution.py:446

commit v2 on v1

--- a/solution.py
+++ b/solution.py
@@ -34,6 +34,28 @@
 
 
 def kernel(
+    levels, experts, per_holder, cuts,
+    grad_hbm, eg_hbm, ew_hbm, w_hbm, m_hbm, v_hbm, hm_hbm, hs_hbm, count_hbm, holder_hbm, slot_hbm, step_hbm,
+    sum_ref, wmv, blocks, scale_ref,
+    grad, pair_out, local, recv, held, mom_out, mom_in, part, parts,
+    count_ref, holder_ref, slot_ref, step_ref,
+):
+    dma = pltpu.SemaphoreType.DMA
+    pl.run_scoped(
+        functools.partial(
+            scoped, levels, experts, per_holder, cuts,
+            grad_hbm, eg_hbm, ew_hbm, w_hbm, m_hbm, v_hbm, hm_hbm, hs_hbm, count_hbm, holder_hbm, slot_hbm, step_hbm,
+            sum_ref, wmv, blocks, scale_ref,
+            grad, pair_out, local, recv, held, mom_out, mom_in, part, parts,
+            count_ref, holder_ref, slot_ref, step_ref,
+        ),
+        dma((levels + 1,)), dma((7,)), dma(()), dma((len(cuts) + levels - 1,)),
+        dma(()), dma((levels + 1, len(cuts))),
+        dma(()), dma(()), dma(()), dma(()),
+    )
+
+
+def scoped(
     levels, experts, per_holder, cuts,
     grad_hbm, eg_hbm, ew_hbm, w_hbm, m_hbm, v_hbm, hm_hbm, hs_hbm, count_hbm, holder_hbm, slot_hbm, step_hbm,
     sum_ref, wmv, blocks, scale_ref,
@@ -409,7 +431,6 @@
         slots = hm.shape[1]
         per_holder = max(1, maxb // experts)
         f32 = jnp.float32
-        dma = pltpu.SemaphoreType.DMA
         hbm = pl.BlockSpec(memory_space=pltpu.HBM)
         vmem = pl.BlockSpec(memory_space=pltpu.VMEM)
         shape = jax.ShapeDtypeStruct
@@ -429,9 +450,6 @@
                 pltpu.VMEM((1, 128), f32), pltpu.VMEM((n_dp * experts, 1, 128), f32),
                 pltpu.SMEM(count.shape, jnp.int32), pltpu.SMEM(holder.shape, jnp.int32),
                 pltpu.SMEM(slot.shape, jnp.int32), pltpu.SMEM(step.shape, jnp.int32),
-                dma((levels + 1,)), dma((7,)), dma(()), dma((len(cuts) + levels - 1,)),
-                dma(()), dma((levels + 1, len(cuts))),
-                dma(()), dma(()), dma(()), dma(()),
             ],
             compiler_params=pltpu.CompilerParams(
                 collective_id=0, has_side_effects=True, vmem_limit_bytes=LIMIT
@@ -448,7 +466,7 @@
             out_shape=[shape((rows, cols), f32)] * 3 + [shape((maxb, width), f32)] * 3,
             in_specs=[vmem] * 4,
             out_specs=[hbm] * 6,
-            scratch_shapes=[pltpu.VMEM((3, rows, cols), f32), pltpu.VMEM((3, maxb, width), f32), dma(()), dma(())],
+            scratch_shapes=[pltpu.VMEM((3, rows, cols), f32), pltpu.VMEM((3, maxb, width), f32), pltpu.SemaphoreType.DMA(()), pltpu.SemaphoreType.DMA(())],
             compiler_params=pltpu.CompilerParams(vmem_limit_bytes=16 * 1024 * 1024),
         )(wmv, sums, blocks, scales)
         return tuple(outs[:3]) + tuple(o[None, None] for o in outs[3:])

time: 66.3 us -> 65.9 us (level)
  no operation moved by 1% of the time
where the time goes in v2:
time: 65.9 us; the launch traced here: 65.8 us
  Pallas kernels  64.5 us (98%)
  between operations  1.28 us (2%)
    pallas_call x1, Pallas kernels, body(): pl.pallas_call(functools.partial(kernel, levels, experts, per_holder, cut...  62.8 us
    pallas_call x1, Pallas kernels, body(): pl.pallas_call(update, out_shape=[shape((rows, cols), f32)] * 3 + [shape(...  1.69 us

profile of v2, /device:TPU:0, one launch (start us, length us, event | category | flops | bytes accessed | tf_op | source)
XLA Modules:
  0.0 65.8 jit_solution(11219550459249782113)
XLA Ops:
  1.3 62.8 %shard_map.163 = (f32[768,256]{1,0:T(8,128)S(1)}, f32[3,768,256]{2,1,0:T(8,128)S(1)}, f32[4,8,6144]{2,1,0:T(8,128)S(1)}, f32[4,128]{1,0:T(4,128)S(1)}) custom-call(bf16[4,2,768,256]{3,2,1,0:T(8,128)(2,1)} %bitcast.8, f32[8,6144]{1,0:T(8,128)} %bitcast.9, f32[8,6144]{1,0:T(8,128)} %bitcast.10, f32[768,256]{1,0:T(8,128)} %w_hbm.1, f32[768,256]{1,0:T(8,128)} %m_hbm.1, ...), custom_call_target="tpu_custom_call" | custom-call | tf_op jit(solution)/shard_map/pallas_call | solution.py:438
  64.1 1.7 %shard_map.164 = (f32[768,256]{1,0:T(8,128)}, f32[768,256]{1,0:T(8,128)}, f32[768,256]{1,0:T(8,128)}, f32[8,6144]{1,0:T(8,128)}, f32[8,6144]{1,0:T(8,128)}, /*index=5*/f32[8,6144]{1,0:T(8,128)}) custom-call(f32[3,768,256]{2,1,0:T(8,128)S(1)} %get-tuple-element.16.wmv, f32[768,256]{1,0:T(8,128)S(1)} %get-tuple-element.17.sums, ...), custom_call_target="tpu_custom_call" | custom-call | tf_op jit(solution)/shard_map/pallas_call | solution.py:464

commit v3 on v2

--- a/solution.py
+++ b/solution.py
@@ -144,13 +144,20 @@
         pair_out[first, spans[p]] = grad[first, other, spans[p]].astype(jnp.float32)
         pair_copy(first, spans[p], p).start()
 
+    def open_link(p):
+        link_copy(way_out, first, p, local.at[first, spans[p]]).start()
+
+    sender = at_end & (first != z)
+    late_core = 1
     for p in range(steps):
         pair_copy(first, spans[p], p).wait_recv()
         local[first, spans[p]] = local[first, spans[p]] + grad[first, core, spans[p]].astype(jnp.float32)
-
-        @pl.when(at_end & (first != z))
-        def _():
-            link_copy(way_out, first, p, local.at[first, spans[p]]).start()
+        if p == 0 and steps > 1:
+            pl.when(sender & (core != late_core))(lambda: open_link(0))
+        elif p == 1:
+            pl.when(sender & (core == late_core))(lambda: open_link(0))
+        if p or steps == 1:
+            pl.when(sender)(lambda: open_link(p))
 
     whole = pl.ds(0, rows)
 
@@ -369,21 +376,22 @@
     second_factor = scale_ref[1:2, 0:1]
     rate = scale_ref[2:3, 0:1]
     epsilon = scale_ref[3:4, 0:1]
-    rows = sums.shape[0]
-    size = chunk_rows(rows)
-
-    @pl.loop(0, rows // size)
-    def _(c):
-        span = pl.ds(pl.multiple_of(c * size, size), size)
+    def chunk(start, size):
+        span = pl.ds(start, size)
         g = sums[span]
         m = wmv[1, span] + first_factor * g
         s = second_factor * g
         v = wmv[2, span] + s * s
         out[1, span] = m
+        pltpu.make_async_copy(out.at[1, span], om_hbm.at[span], sem).start()
         out[2, span] = v
+        pltpu.make_async_copy(out.at[2, span], ov_hbm.at[span], sem).start()
         out[0, span] = wmv[0, span] - rate * m / (v * lax.rsqrt(v) + epsilon)
-        for i, dst in enumerate((ow_hbm, om_hbm, ov_hbm)):
-            pltpu.make_async_copy(out.at[i, span], dst.at[span], sem).start()
+        pltpu.make_async_copy(out.at[0, span], ow_hbm.at[span], sem).start()
+
+    rows = sums.shape[0]
+    for start, size in chunk_rows(rows):
+        chunk(start, size)
 
     width = blocks.shape[2]
     for i in range(width // 128):
@@ -402,10 +410,11 @@
 
 
 def chunk_rows(rows):
-    for size in range(96, 0, -8):
-        if rows % size == 0:
-            return size
-    return rows
+    unit = rows // 8 // 8 * 8
+    if not unit or rows % 8:
+        return ((0, rows),)
+    sizes = [unit, 2 * unit, 2 * unit, rows - 5 * unit]
+    return tuple((sum(sizes[:i]), sizes[i]) for i in range(4))
 
 
 def cut_rows(rows):

time: 65.9 us -> 65.5 us (level)
  no operation moved by 1% of the time
where the time goes in v3:
time: 65.5 us; the launch traced here: 65.4 us
  Pallas kernels  64.1 us (98%)
  between operations  1.28 us (2%)
    pallas_call x1, Pallas kernels, body(): pl.pallas_call(functools.partial(kernel, levels, experts, per_holder, cut...  62.4 us
    pallas_call x1, Pallas kernels, body(): pl.pallas_call(update, out_shape=[shape((rows, cols), f32)] * 3 + [shape(...  1.66 us

profile of v3, /device:TPU:0, one launch (start us, length us, event | category | flops | bytes accessed | tf_op | source)
XLA Modules:
  0.0 65.4 jit_solution(2983695350960733566)
XLA Ops:
  1.3 62.4 %shard_map.163 = (f32[768,256]{1,0:T(8,128)S(1)}, f32[3,768,256]{2,1,0:T(8,128)S(1)}, f32[4,8,6144]{2,1,0:T(8,128)S(1)}, f32[4,128]{1,0:T(4,128)S(1)}) custom-call(bf16[4,2,768,256]{3,2,1,0:T(8,128)(2,1)} %bitcast.8, f32[8,6144]{1,0:T(8,128)} %bitcast.9, f32[8,6144]{1,0:T(8,128)} %bitcast.10, f32[768,256]{1,0:T(8,128)} %w_hbm.1, f32[768,256]{1,0:T(8,128)} %m_hbm.1, ...), custom_call_target="tpu_custom_call" | custom-call | tf_op jit(solution)/shard_map/pallas_call | solution.py:447
  63.7 1.7 %shard_map.164 = (f32[768,256]{1,0:T(8,128)}, f32[768,256]{1,0:T(8,128)}, f32[768,256]{1,0:T(8,128)}, f32[8,6144]{1,0:T(8,128)}, f32[8,6144]{1,0:T(8,128)}, /*index=5*/f32[8,6144]{1,0:T(8,128)}) custom-call(f32[3,768,256]{2,1,0:T(8,128)S(1)} %get-tuple-element.16.wmv, f32[768,256]{1,0:T(8,128)S(1)} %get-tuple-element.17.sums, ...), custom_call_target="tpu_custom_call" | custom-call | tf_op jit(solution)/shard_map/pallas_call | solution.py:473

commit v4 on v3

--- a/solution.py
+++ b/solution.py
@@ -37,7 +37,7 @@
     levels, experts, per_holder, cuts,
     grad_hbm, eg_hbm, ew_hbm, w_hbm, m_hbm, v_hbm, hm_hbm, hs_hbm, count_hbm, holder_hbm, slot_hbm, step_hbm,
     sum_ref, wmv, blocks, scale_ref,
-    grad, pair_out, local, recv, held, mom_out, mom_in, part, parts,
+    grad, pair_out, local, recv, held, mom_out, mom_in, part, parts, edge_part,
     count_ref, holder_ref, slot_ref, step_ref,
 ):
     dma = pltpu.SemaphoreType.DMA
@@ -46,12 +46,12 @@
             scoped, levels, experts, per_holder, cuts,
             grad_hbm, eg_hbm, ew_hbm, w_hbm, m_hbm, v_hbm, hm_hbm, hs_hbm, count_hbm, holder_hbm, slot_hbm, step_hbm,
             sum_ref, wmv, blocks, scale_ref,
-            grad, pair_out, local, recv, held, mom_out, mom_in, part, parts,
+            grad, pair_out, local, recv, held, mom_out, mom_in, part, parts, edge_part,
             count_ref, holder_ref, slot_ref, step_ref,
         ),
         dma((levels + 1,)), dma((7,)), dma(()), dma((len(cuts) + levels - 1,)),
         dma(()), dma((levels + 1, len(cuts))),
-        dma(()), dma(()), dma(()), dma(()),
+        dma(()), dma(()), dma(()), dma(()), dma(()), dma((2,)),
     )
 
 
@@ -59,10 +59,10 @@
     levels, experts, per_holder, cuts,
     grad_hbm, eg_hbm, ew_hbm, w_hbm, m_hbm, v_hbm, hm_hbm, hs_hbm, count_hbm, holder_hbm, slot_hbm, step_hbm,
     sum_ref, wmv, blocks, scale_ref,
-    grad, pair_out, local, recv, held, mom_out, mom_in, part, parts,
+    grad, pair_out, local, recv, held, mom_out, mom_in, part, parts, edge_part,
     count_ref, holder_ref, slot_ref, step_ref,
     grad_sem, load_sem, pair_send, pair_recv, link_send, link_recv,
-    mom_send, mom_recv, part_send, part_recv,
+    mom_send, mom_recv, part_send, part_recv, back_send, edge_sem,
 ):
     dp = lax.axis_index("dp")
     me = lax.axis_index("expert")
@@ -76,6 +76,8 @@
     steps = len(cuts)
     devices = levels * CORES * experts
     spans = [pl.ds(start, size) for start, size in cuts]
+    kept = sum(start + size <= rows // 2 for start, size in cuts) if levels >= 4 else 0
+    near = ((z == 1) | (z == levels - 2)) if kept else False
 
     def level_of(j):
         return jnp.where(upper, j, levels - 1 - j)
@@ -122,11 +124,11 @@
             device_id=(partner, me), device_id_type=MESH,
         )
 
-    def link_copy(way, d, p, src):
+    def link_copy(way, d, p, src, send=link_send):
         slot = d + 1 - way
         return pltpu.make_async_remote_copy(
             src_ref=src, dst_ref=recv.at[slot, spans[p]],
-            send_sem=link_send, recv_sem=link_recv.at[slot, p],
+            send_sem=send, recv_sem=link_recv.at[slot, p],
             device_id=(jnp.where(way == 0, dp + CORES, dp - CORES), me), device_id_type=MESH,
         )
 
@@ -135,8 +137,8 @@
 
     opening[0].wait()
     pair_out[first, spans[0]] = grad[first, other, spans[0]].astype(jnp.float32)
-    near = jnp.where(z > 0, 1, 0) + jnp.where(z < levels - 1, 1, 0)
-    pl.semaphore_wait(barrier, experts + near)
+    linked = jnp.where(z > 0, 1, 0) + jnp.where(z < levels - 1, 1, 0)
+    pl.semaphore_wait(barrier, experts + linked)
     pair_copy(first, spans[0], 0).start()
     for load in opening[1:]:
         load.wait()
@@ -149,14 +151,18 @@
 
     sender = at_end & (first != z)
     late_core = 1
+    hold = min(3, steps - 1)
     for p in range(steps):
         pair_copy(first, spans[p], p).wait_recv()
         local[first, spans[p]] = local[first, spans[p]] + grad[first, core, spans[p]].astype(jnp.float32)
-        if p == 0 and steps > 1:
+        if p == 0 and hold:
             pl.when(sender & (core != late_core))(lambda: open_link(0))
-        elif p == 1:
-            pl.when(sender & (core == late_core))(lambda: open_link(0))
-        if p or steps == 1:
+        if p == hold and hold:
+            for q in range(hold):
+                pl.when(sender & (core == late_core))(lambda: open_link(q))
+        if 0 < p < hold:
+            pl.when(sender & (core != late_core))(lambda: open_link(p))
+        elif p >= hold:
             pl.when(sender)(lambda: open_link(p))
 
     whole = pl.ds(0, rows)
@@ -179,7 +185,7 @@
 
         @pl.when(at_end & (j == levels - 2))
         def _():
-            for p in reversed(range(steps)):
+            for p in reversed(range(kept, steps)):
                 link_copy(way_out, d, p, local.at[d, spans[p]]).start()
 
     ints = [
@@ -251,6 +257,14 @@
             copy.wait_recv()
             recv[slot, spans[p]] = recv[slot, spans[p]] + local[d, spans[p]]
             copy.start()
+
+        if p < kept:
+            @pl.when((d == z) & (z == jnp.where(way == 0, levels - 2, 1)))
+            def _():
+                copy = link_copy(way, d, p, recv.at[slot, spans[p]], back_send)
+                copy.wait_recv()
+                recv[slot, spans[p]] = recv[slot, spans[p]] + local[d, spans[p]]
+                copy.start()
 
     @pl.loop(0, levels)
     def _(j):
@@ -308,8 +322,18 @@
     early = 1 - way_out
     inner = jnp.where(upper, z > 0, z < levels - 1)
     outer = jnp.where(upper, z < levels - 1, z > 0)
+    part[...] = row
+
+    def square(ref, at):
+        g = ref[at]
+        col = jnp.sum(g * g, axis=0, keepdims=True)
+        for i in range(g.shape[1] // 128):
+            part[...] = part[...] + col[:, i * 128:(i + 1) * 128]
+
     for p in range(steps):
-        @pl.when(inner)
+        taken = near if p < kept else False
+
+        @pl.when(inner & jnp.logical_not(taken))
         def _():
             link_copy(early, z, p, recv.at[z + 1 - early, spans[p]]).wait_recv()
             sum_ref[spans[p]] = local[z, spans[p]] + recv[z + 1 - early, spans[p]]
@@ -318,20 +342,34 @@
         def _():
             sum_ref[spans[p]] = local[z, spans[p]]
 
+    if kept:
+        @pl.when(at_end)
+        def _():
+            d = level_of(levels - 2)
+            slot = d + 1 - early
+            for p in range(kept):
+                block = recv.at[slot, spans[p]]
+                link_copy(early, d, p, block).wait_recv()
+                recv[slot, spans[p]] = recv[slot, spans[p]] + local[d, spans[p]]
+                square(recv, (slot, spans[p]))
+
+    def last(p):
+        link_copy(way_out, z, p, recv.at[z + 1 - way_out, spans[p]]).wait_recv()
+
     for p in reversed(range(steps)):
-        @pl.when(outer)
-        def _():
-            link_copy(way_out, z, p, recv.at[z + 1 - way_out, spans[p]]).wait_recv()
+        taken = near if p < kept else False
+
+        @pl.when(outer & jnp.logical_not(taken))
+        def _():
+            last(p)
             sum_ref[spans[p]] = sum_ref[spans[p]] + recv[z + 1 - way_out, spans[p]]
 
-        g = sum_ref[spans[p]]
-        col = jnp.sum(g * g, axis=0, keepdims=True)
-        for i in range(g.shape[1] // 128):
-            row = row + col[:, i * 128:(i + 1) * 128]
-
-    index = dp * experts + me
-    part[...] = row
-    parts[index] = row
+        @pl.when(jnp.logical_not(taken))
+        def _():
+            square(sum_ref, spans[p])
+
+    inside = devices - 2 * CORES * experts if kept else devices
+    index = dp * experts + me - (CORES * experts if kept else 0)
 
     def part_copy(target_dp, target_me):
         return pltpu.make_async_remote_copy(
@@ -340,28 +378,74 @@
             device_id=(target_dp, target_me), device_id_type=MESH,
         )
 
-    if devices <= 64:
-        for far in far_first(levels):
-            side = lax.rem(z + far, levels) * CORES
-            for off in far_first(experts):
-                target = lax.rem(me + off, experts)
-                for swap in range(CORES):
-                    if far or off or swap:
-                        part_copy(side + lax.rem(core + swap, CORES), target).start()
+    def spread():
+        parts[index] = part[...]
+        if devices <= 64:
+            for far in far_first(levels):
+                side = lax.rem(z + far, levels) * CORES
+                for off in far_first(experts):
+                    target = lax.rem(me + off, experts)
+                    for swap in range(CORES):
+                        if far or off or swap:
+                            part_copy(side + lax.rem(core + swap, CORES), target).start()
+        else:
+            @pl.loop(1, devices)
+            def _(off):
+                target = lax.rem(dp * experts + me + off, devices)
+                part_copy(target // experts, lax.rem(target, experts)).start()
+
+    everyone = parts.at[pl.ds(0, devices - 1)]
+    if kept:
+        edge = pltpu.make_async_remote_copy(
+            src_ref=part, dst_ref=edge_part, send_sem=edge_sem.at[0], recv_sem=edge_sem.at[1],
+            device_id=(jnp.where(upper, dp - CORES, dp + CORES), me), device_id_type=MESH,
+        )
+
+        @pl.when(at_end)
+        def _():
+            edge.start()
+            d = level_of(levels - 2)
+            for p in reversed(range(kept)):
+                link_copy(way_out, d, p, recv.at[d + 1 - early, spans[p]]).start()
+
+        @pl.when(near)
+        def _():
+            edge.wait_recv()
+            part[...] = part[...] + edge_part[...]
+
+        pl.when(jnp.logical_not(at_end))(spread)
     else:
-        @pl.loop(1, devices)
-        def _(off):
-            target = lax.rem(index + off, devices)
-            part_copy(target // experts, lax.rem(target, experts)).start()
+        spread()
+
+    if kept:
+        @pl.when(near)
+        def _():
+            for p in reversed(range(kept)):
+                last(p)
+                sum_ref[spans[p]] = recv[z + 1 - way_out, spans[p]]
+            back = local.at[0, pl.ds(0, sum(size for _, size in cuts[:kept]))]
+            pltpu.make_async_copy(back, back, back_send).wait()
 
     pltpu.make_async_copy(pair_out, pair_out, pair_send).wait()
     if levels > 1:
         sent = local.at[pl.ds(0, levels - 1)]
         pltpu.make_async_copy(sent, sent, link_send).wait()
-    others = parts.at[pl.ds(0, devices - 1)]
-    pltpu.make_async_copy(others, others, part_send).wait()
-    pltpu.make_async_copy(others, others, part_recv).wait()
-    total = jnp.sum(jnp.sum(parts[...], axis=0), axis=1, keepdims=True)
+    if kept:
+        @pl.when(at_end)
+        def _():
+            edge.wait_send()
+            everything = parts.at[pl.ds(0, inside)]
+            pltpu.make_async_copy(everything, everything, part_recv).wait()
+
+        @pl.when(jnp.logical_not(at_end))
+        def _():
+            pltpu.make_async_copy(everyone, everyone, part_send).wait()
+            others = parts.at[pl.ds(0, inside - 1)]
+            pltpu.make_async_copy(others, others, part_recv).wait()
+    else:
+        pltpu.make_async_copy(everyone, everyone, part_send).wait()
+        pltpu.make_async_copy(everyone, everyone, part_recv).wait()
+    total = jnp.sum(jnp.sum(parts[pl.ds(0, inside)], axis=0), axis=1, keepdims=True)
     factor = jnp.broadcast_to(jnp.minimum(1.0, clip_norm / (jnp.sqrt(total) + 1e-06)), (1, 128))
     scale_ref[0:1] = (1.0 - beta_first) * factor
     scale_ref[1:2] = (1.0 - beta_second) ** 0.5 * factor
@@ -418,13 +502,14 @@
 
 
 def cut_rows(rows):
-    if rows % 16:
+    unit = rows // 6 // 16 * 16
+    if not unit or rows % 16:
         return ((0, rows),)
-    head = max(16, rows // 12 // 16 * 16)
-    half = (rows - head) // 2 // 16 * 16
-    sizes = [size for size in (head, half, rows - head - half) if size > 0]
-    starts = [sum(sizes[:i]) for i in range(len(sizes))]
-    return tuple(zip(starts, sizes))
+    half = unit // 2 // 16 * 16
+    sizes = ([half, unit - half] if half else [unit]) + [unit] * ((rows - unit) // unit)
+    if rows > sum(sizes):
+        sizes.append(rows - sum(sizes))
+    return tuple((sum(sizes[:i]), sizes[i]) for i in range(len(sizes)))
 
 
 def make_body(mesh):
@@ -456,7 +541,7 @@
                 pltpu.VMEM((levels + 1, rows, cols), f32),
                 pltpu.VMEM((2, slots, width), f32),
                 pltpu.VMEM(moved, f32), pltpu.VMEM(moved, f32),
-                pltpu.VMEM((1, 128), f32), pltpu.VMEM((n_dp * experts, 1, 128), f32),
+                pltpu.VMEM((1, 128), f32), pltpu.VMEM((n_dp * experts, 1, 128), f32), pltpu.VMEM((1, 128), f32),
                 pltpu.SMEM(count.shape, jnp.int32), pltpu.SMEM(holder.shape, jnp.int32),
                 pltpu.SMEM(slot.shape, jnp.int32), pltpu.SMEM(step.shape, jnp.int32),
             ],

time: 65.5 us -> 59.7 us (0.911)
  the two profiles are of different devices: /device:TPU:0 before, /device:TPU:17 now
where the time goes in v4:
time: 59.7 us; the launch traced here: 59.6 us
  Pallas kernels  58.3 us (98%)
  between operations  1.28 us (2%)
    pallas_call x1, Pallas kernels, body(): pl.pallas_call(functools.partial(kernel, levels, experts, per_holder, cut...  56.6 us
    pallas_call x1, Pallas kernels, body(): pl.pallas_call(update, out_shape=[shape((rows, cols), f32)] * 3 + [shape(...  1.66 us

profile of v4, /device:TPU:17, one launch (start us, length us, event | category | flops | bytes accessed | tf_op | source)
XLA Modules:
  0.0 59.6 jit_solution(7854881027478141873)
XLA Ops:
  1.3 56.6 %shard_map.163 = (f32[768,256]{1,0:T(8,128)S(1)}, f32[3,768,256]{2,1,0:T(8,128)S(1)}, f32[4,8,6144]{2,1,0:T(8,128)S(1)}, f32[4,128]{1,0:T(4,128)S(1)}) custom-call(bf16[4,2,768,256]{3,2,1,0:T(8,128)(2,1)} %bitcast.8, f32[8,6144]{1,0:T(8,128)} %bitcast.9, f32[8,6144]{1,0:T(8,128)} %bitcast.10, f32[768,256]{1,0:T(8,128)} %w_hbm.1, f32[768,256]{1,0:T(8,128)} %m_hbm.1, ...), custom_call_target="tpu_custom_call" | custom-call | tf_op jit(solution)/shard_map/pallas_call | solution.py:532
  57.9 1.7 %shard_map.164 = (f32[768,256]{1,0:T(8,128)}, f32[768,256]{1,0:T(8,128)}, f32[768,256]{1,0:T(8,128)}, f32[8,6144]{1,0:T(8,128)}, f32[8,6144]{1,0:T(8,128)}, /*index=5*/f32[8,6144]{1,0:T(8,128)}) custom-call(f32[3,768,256]{2,1,0:T(8,128)S(1)} %get-tuple-element.16.wmv, f32[768,256]{1,0:T(8,128)S(1)} %get-tuple-element.17.sums, ...), custom_call_target="tpu_custom_call" | custom-call | tf_op jit(solution)/shard_map/pallas_call | solution.py:558

commit v5 on v4

--- a/solution.py
+++ b/solution.py
@@ -9,6 +9,7 @@
 
 MESH = pl.DeviceIdType.MESH
 CORES = 2
+WRITES = 4
 LIMIT = 40 * 1024 * 1024
 
 beta_first = 0.9
@@ -36,8 +37,8 @@
 def kernel(
     levels, experts, per_holder, cuts,
     grad_hbm, eg_hbm, ew_hbm, w_hbm, m_hbm, v_hbm, hm_hbm, hs_hbm, count_hbm, holder_hbm, slot_hbm, step_hbm,
-    sum_ref, wmv, blocks, scale_ref,
-    grad, pair_out, local, recv, held, mom_out, mom_in, part, parts, edge_part,
+    wmv, blocks,
+    sum_ref, scale_ref, grad, pair_out, local, recv, held, mom_out, mom_in, part, parts, edge_part,
     count_ref, holder_ref, slot_ref, step_ref,
 ):
     dma = pltpu.SemaphoreType.DMA
@@ -45,24 +46,25 @@
         functools.partial(
             scoped, levels, experts, per_holder, cuts,
             grad_hbm, eg_hbm, ew_hbm, w_hbm, m_hbm, v_hbm, hm_hbm, hs_hbm, count_hbm, holder_hbm, slot_hbm, step_hbm,
-            sum_ref, wmv, blocks, scale_ref,
-            grad, pair_out, local, recv, held, mom_out, mom_in, part, parts, edge_part,
+            wmv, blocks,
+            sum_ref, scale_ref, grad, pair_out, local, recv, held, mom_out, mom_in, part, parts, edge_part,
             count_ref, holder_ref, slot_ref, step_ref,
         ),
         dma((levels + 1,)), dma((7,)), dma(()), dma((len(cuts) + levels - 1,)),
         dma(()), dma((levels + 1, len(cuts))),
         dma(()), dma(()), dma(()), dma(()), dma(()), dma((2,)),
+        pltpu.SemaphoreType.REGULAR, pltpu.SemaphoreType.REGULAR,
     )
 
 
 def scoped(
     levels, experts, per_holder, cuts,
     grad_hbm, eg_hbm, ew_hbm, w_hbm, m_hbm, v_hbm, hm_hbm, hs_hbm, count_hbm, holder_hbm, slot_hbm, step_hbm,
-    sum_ref, wmv, blocks, scale_ref,
-    grad, pair_out, local, recv, held, mom_out, mom_in, part, parts, edge_part,
+    wmv, blocks,
+    sum_ref, scale_ref, grad, pair_out, local, recv, held, mom_out, mom_in, part, parts, edge_part,
     count_ref, holder_ref, slot_ref, step_ref,
     grad_sem, load_sem, pair_send, pair_recv, link_send, link_recv,
-    mom_send, mom_recv, part_send, part_recv, back_send, edge_sem,
+    mom_send, mom_recv, part_send, part_recv, back_send, edge_sem, ready_sem, open_sem,
 ):
     dp = lax.axis_index("dp")
     me = lax.axis_index("expert")
@@ -98,6 +100,7 @@
         opening.append(load_first(levels, head, rows - head))
     opening[0].start()
 
+    at_end = (z == 0) | (z == levels - 1)
     barrier = pltpu.get_barrier_semaphore()
     pl.semaphore_signal(barrier, inc=1, device_id=(partner, me), device_id_type=MESH)
 
@@ -109,8 +112,14 @@
     def _():
         pl.semaphore_signal(barrier, inc=1, device_id=(dp + CORES, me), device_id_type=MESH)
 
-    for off in range(1, experts):
-        pl.semaphore_signal(barrier, inc=1, device_id=(dp, lax.rem(me + off, experts)), device_id_type=MESH)
+    def greet(sem):
+        for off in range(1, experts):
+            pl.semaphore_signal(sem, inc=1, device_id=(dp, lax.rem(me + off, experts)), device_id_type=MESH)
+
+    if kept:
+        pl.when(jnp.logical_not(at_end))(lambda: greet(barrier))
+    else:
+        greet(barrier)
 
     for load in opening[1:]:
         load.start()
@@ -133,12 +142,12 @@
         )
 
     way_out = jnp.where(upper, 1, 0)
-    at_end = (z == 0) | (z == levels - 1)
 
     opening[0].wait()
     pair_out[first, spans[0]] = grad[first, other, spans[0]].astype(jnp.float32)
     linked = jnp.where(z > 0, 1, 0) + jnp.where(z < levels - 1, 1, 0)
-    pl.semaphore_wait(barrier, experts + linked)
+    crossed = jnp.where(at_end, 0, experts - 1) if kept else experts - 1
+    pl.semaphore_wait(barrier, 1 + linked + crossed)
     pair_copy(first, spans[0], 0).start()
     for load in opening[1:]:
         load.wait()
@@ -208,6 +217,8 @@
 
         take(j)
 
+    if kept:
+        pl.when(near)(lambda: greet(ready_sem))
     for i, source in enumerate((w_hbm, m_hbm, v_hbm)):
         pltpu.make_async_copy(source, wmv.at[i], load_sem.at[5]).start()
     for i, source in enumerate((eg_hbm, ew_hbm)):
@@ -232,6 +243,17 @@
                 chosen[q] = jnp.where(mine & (rank == q), slot_ref[owner, b], chosen[q])
             rank = rank + jnp.where(mine, 1, 0)
         return chosen
+
+    if kept:
+        @pl.when(near)
+        def _():
+            pl.semaphore_wait(ready_sem, experts - 1)
+            edge_dp = jnp.where(upper, dp + CORES, dp - CORES)
+            pl.semaphore_signal(open_sem, inc=1, device_id=(edge_dp, me), device_id_type=MESH)
+
+        @pl.when(at_end)
+        def _():
+            pl.semaphore_wait(open_sem, 1)
 
     for q, slot in enumerate(picks(me)):
         for i in range(2):
@@ -394,7 +416,6 @@
                 target = lax.rem(dp * experts + me + off, devices)
                 part_copy(target // experts, lax.rem(target, experts)).start()
 
-    everyone = parts.at[pl.ds(0, devices - 1)]
     if kept:
         edge = pltpu.make_async_remote_copy(
             src_ref=part, dst_ref=edge_part, send_sem=edge_sem.at[0], recv_sem=edge_sem.at[1],
@@ -417,88 +438,84 @@
     else:
         spread()
 
-    if kept:
-        @pl.when(near)
-        def _():
-            for p in reversed(range(kept)):
-                last(p)
-                sum_ref[spans[p]] = recv[z + 1 - way_out, spans[p]]
-            back = local.at[0, pl.ds(0, sum(size for _, size in cuts[:kept]))]
-            pltpu.make_async_copy(back, back, back_send).wait()
-
-    pltpu.make_async_copy(pair_out, pair_out, pair_send).wait()
-    if levels > 1:
-        sent = local.at[pl.ds(0, levels - 1)]
-        pltpu.make_async_copy(sent, sent, link_send).wait()
+    everyone = parts.at[pl.ds(0, devices - 1)]
     if kept:
         @pl.when(at_end)
         def _():
-            edge.wait_send()
             everything = parts.at[pl.ds(0, inside)]
             pltpu.make_async_copy(everything, everything, part_recv).wait()
 
         @pl.when(jnp.logical_not(at_end))
         def _():
-            pltpu.make_async_copy(everyone, everyone, part_send).wait()
             others = parts.at[pl.ds(0, inside - 1)]
             pltpu.make_async_copy(others, others, part_recv).wait()
     else:
-        pltpu.make_async_copy(everyone, everyone, part_send).wait()
         pltpu.make_async_copy(everyone, everyone, part_recv).wait()
     total = jnp.sum(jnp.sum(parts[pl.ds(0, inside)], axis=0), axis=1, keepdims=True)
     factor = jnp.broadcast_to(jnp.minimum(1.0, clip_norm / (jnp.sqrt(total) + 1e-06)), (1, 128))
     scale_ref[0:1] = (1.0 - beta_first) * factor
     scale_ref[1:2] = (1.0 - beta_second) ** 0.5 * factor
 
-
-def update(
-    wmv, sums, blocks, scale_ref,
-    ow_hbm, om_hbm, ov_hbm, oew_hbm, oem_hbm, oes_hbm,
-    out, block_out, sem, block_sem,
-):
-    first_factor = scale_ref[0:1, 0:1]
-    second_factor = scale_ref[1:2, 0:1]
-    rate = scale_ref[2:3, 0:1]
-    epsilon = scale_ref[3:4, 0:1]
-    def chunk(start, size):
-        span = pl.ds(start, size)
-        g = sums[span]
-        m = wmv[1, span] + first_factor * g
-        s = second_factor * g
+    def finish(span, g):
+        m = wmv[1, span] + scale_ref[0:1, 0:1] * g
+        s = scale_ref[1:2, 0:1] * g
         v = wmv[2, span] + s * s
-        out[1, span] = m
-        pltpu.make_async_copy(out.at[1, span], om_hbm.at[span], sem).start()
-        out[2, span] = v
-        pltpu.make_async_copy(out.at[2, span], ov_hbm.at[span], sem).start()
-        out[0, span] = wmv[0, span] - rate * m / (v * lax.rsqrt(v) + epsilon)
-        pltpu.make_async_copy(out.at[0, span], ow_hbm.at[span], sem).start()
-
-    rows = sums.shape[0]
-    for start, size in chunk_rows(rows):
-        chunk(start, size)
-
-    width = blocks.shape[2]
+        wmv[1, span] = m
+        wmv[2, span] = v
+        wmv[0, span] = wmv[0, span] - scale_ref[2:3, 0:1] * m / (v * lax.rsqrt(v) + scale_ref[3:4, 0:1])
+
+    for p in range(kept, steps):
+        finish(spans[p], sum_ref[spans[p]])
     for i in range(width // 128):
-        cols = pl.ds(i * 128, 128)
-        g = blocks[0, :, cols]
-        m = blocks[2, :, cols] + first_factor * g
-        s = second_factor * g
-        v = blocks[3, :, cols] + s * s
-        block_out[1, :, cols] = m
-        block_out[2, :, cols] = v
-        block_out[0, :, cols] = blocks[1, :, cols] - rate * m / (jnp.sqrt(v) + epsilon)
+        span = pl.ds(i * 128, 128)
+        g = blocks[0, :, span]
+        m = blocks[2, :, span] + scale_ref[0:1, 0:1] * g
+        s = scale_ref[1:2, 0:1] * g
+        v = blocks[3, :, span] + s * s
+        blocks[2, :, span] = m
+        blocks[3, :, span] = v
+        blocks[1, :, span] = blocks[1, :, span] - scale_ref[2:3, 0:1] * m / (jnp.sqrt(v) + scale_ref[3:4, 0:1])
+    if kept:
+        @pl.when(jnp.logical_not(near))
+        def _():
+            for p in range(kept):
+                finish(spans[p], sum_ref[spans[p]])
+
+    pltpu.make_async_copy(pair_out, pair_out, pair_send).wait()
+    if levels > 1:
+        sent = local.at[pl.ds(0, levels - 1)]
+        pltpu.make_async_copy(sent, sent, link_send).wait()
+    if kept:
+        @pl.when(at_end)
+        def _():
+            edge.wait_send()
+
+        @pl.when(jnp.logical_not(at_end))
+        def _():
+            pltpu.make_async_copy(everyone, everyone, part_send).wait()
+
+        @pl.when(near)
+        def _():
+            back = local.at[0, pl.ds(0, sum(size for _, size in cuts[:kept]))]
+            pltpu.make_async_copy(back, back, back_send).wait()
+            for p in reversed(range(kept)):
+                last(p)
+                finish(spans[p], recv[z + 1 - way_out, spans[p]])
+    else:
+        pltpu.make_async_copy(everyone, everyone, part_send).wait()
+
+
+def write(parts, wmv, blocks, ow_hbm, om_hbm, ov_hbm, oew_hbm, oem_hbm, oes_hbm, sem, block_sem):
+    size = wmv.shape[1] // parts
+    for k in range(parts):
+        span = pl.ds(k * size, size)
+        for i, dst in enumerate((ow_hbm, om_hbm, ov_hbm)):
+            pltpu.make_async_copy(wmv.at[i, span], dst.at[span], sem).start()
     for i, dst in enumerate((oew_hbm, oem_hbm, oes_hbm)):
-        pltpu.make_async_copy(block_out.at[i], dst, block_sem).start()
-    pltpu.make_async_copy(out, out, sem).wait()
-    pltpu.make_async_copy(block_out, block_out, block_sem).wait()
-
-
-def chunk_rows(rows):
-    unit = rows // 8 // 8 * 8
-    if not unit or rows % 8:
-        return ((0, rows),)
-    sizes = [unit, 2 * unit, 2 * unit, rows - 5 * unit]
-    return tuple((sum(sizes[:i]), sizes[i]) for i in range(4))
+        pltpu.make_async_copy(blocks.at[i + 1], dst, block_sem).start()
+    done = blocks.at[pl.ds(1, 3)]
+    pltpu.make_async_copy(wmv, wmv, sem).wait()
+    pltpu.make_async_copy(done, done, block_sem).wait()
 
 
 def cut_rows(rows):
@@ -529,12 +546,13 @@
         vmem = pl.BlockSpec(memory_space=pltpu.VMEM)
         shape = jax.ShapeDtypeStruct
         moved = (experts, 2, per_holder, width)
-        sums, wmv, blocks, scales = pl.pallas_call(
+        wmv, blocks = pl.pallas_call(
             functools.partial(kernel, levels, experts, per_holder, cuts),
-            out_shape=[pltpu.VMEM(s, f32) for s in ((rows, cols), (3, rows, cols), (4, maxb, width), (4, 128))],
+            out_shape=[pltpu.VMEM(s, f32) for s in ((3, rows, cols), (4, maxb, width))],
             in_specs=[hbm] * 12,
-            out_specs=[vmem] * 4,
+            out_specs=[vmem] * 2,
             scratch_shapes=[
+                pltpu.VMEM((rows, cols), f32), pltpu.VMEM((4, 128), f32),
                 pltpu.VMEM((levels, CORES, rows, cols), ag.dtype),
                 pltpu.VMEM((levels, rows, cols), f32),
                 pltpu.VMEM((levels, rows, cols), f32),
@@ -556,13 +574,13 @@
             step,
         )
         outs = pl.pallas_call(
-            update,
+            functools.partial(write, WRITES if rows % (8 * WRITES) == 0 else 1),
             out_shape=[shape((rows, cols), f32)] * 3 + [shape((maxb, width), f32)] * 3,
-            in_specs=[vmem] * 4,
+            in_specs=[vmem] * 2,
             out_specs=[hbm] * 6,
-            scratch_shapes=[pltpu.VMEM((3, rows, cols), f32), pltpu.VMEM((3, maxb, width), f32), pltpu.SemaphoreType.DMA(()), pltpu.SemaphoreType.DMA(())],
+            scratch_shapes=[pltpu.SemaphoreType.DMA(()), pltpu.SemaphoreType.DMA(())],
             compiler_params=pltpu.CompilerParams(vmem_limit_bytes=16 * 1024 * 1024),
-        )(wmv, sums, blocks, scales)
+        )(wmv, blocks)
         return tuple(outs[:3]) + tuple(o[None, None] for o in outs[3:])
 
     return body

time: 59.7 us -> 58.4 us (0.978)
  the two profiles are of different devices: /device:TPU:17 before, /device:TPU:0 now
where the time goes in v5:
time: 58.4 us; the launch traced here: 58 us
  Pallas kernels  56.7 us (97%)
  between operations  1.28 us (2%)
    pallas_call x1, Pallas kernels, body(): pl.pallas_call(functools.partial(kernel, levels, experts, per_holder, cut...  55.1 us
    pallas_call x1, Pallas kernels, body(): pl.pallas_call(functools.partial(write, WRITES if rows % (8 * WRITES) ==...  1.59 us

profile of v5, /device:TPU:0, one launch (start us, length us, event | category | flops | bytes accessed | tf_op | source)
XLA Modules:
  0.0 58.0 jit_solution(6860263883515498574)
XLA Ops:
  1.3 55.1 %shard_map.163 = (f32[3,768,256]{2,1,0:T(8,128)S(1)}, f32[4,8,6144]{2,1,0:T(8,128)S(1)}) custom-call(bf16[4,2,768,256]{3,2,1,0:T(8,128)(2,1)} %bitcast.8, f32[8,6144]{1,0:T(8,128)} %bitcast.9, f32[8,6144]{1,0:T(8,128)} %bitcast.10, f32[768,256]{1,0:T(8,128)} %w_hbm.1, f32[768,256]{1,0:T(8,128)} %m_hbm.1, f32[768,256]{1,0:T(8,128)} %v_hbm.1, ...), custom_call_target="tpu_custom_call" | custom-call | tf_op jit(solution)/shard_map/pallas_call | solution.py:549
  56.4 1.6 %shard_map.164 = (f32[768,256]{1,0:T(8,128)}, f32[768,256]{1,0:T(8,128)}, f32[768,256]{1,0:T(8,128)}, f32[8,6144]{1,0:T(8,128)}, f32[8,6144]{1,0:T(8,128)}, /*index=5*/f32[8,6144]{1,0:T(8,128)}) custom-call(f32[3,768,256]{2,1,0:T(8,128)S(1)} %get-tuple-element.14.wmv, f32[4,8,6144]{2,1,0:T(8,128)S(1)} %get-tuple-element.15.blocks), custom_call_target="tpu_custom_call" | custom-call | tf_op jit(solution)/shard_map/pallas_call | solution.py:576

commit v6 on v5

--- a/solution.py
+++ b/solution.py
@@ -10,6 +10,7 @@
 MESH = pl.DeviceIdType.MESH
 CORES = 2
 WRITES = 4
+LAG = 2
 LIMIT = 40 * 1024 * 1024
 
 beta_first = 0.9
@@ -160,7 +161,7 @@
 
     sender = at_end & (first != z)
     late_core = 1
-    hold = min(3, steps - 1)
+    hold = min(2, steps - 1)
     for p in range(steps):
         pair_copy(first, spans[p], p).wait_recv()
         local[first, spans[p]] = local[first, spans[p]] + grad[first, core, spans[p]].astype(jnp.float32)
@@ -288,18 +289,18 @@
                 recv[slot, spans[p]] = recv[slot, spans[p]] + local[d, spans[p]]
                 copy.start()
 
+    lag = min(LAG, steps)
+
     @pl.loop(0, levels)
     def _(j):
         for p in range(steps):
             forward(way_out, j, p)
-            if p:
-                forward(1 - way_out, j, p - 1)
+            if p >= lag:
+                forward(1 - way_out, j, p - lag)
             else:
                 @pl.when(j > 0)
                 def _():
-                    forward(1 - way_out, j - 1, steps - 1)
-
-    forward(1 - way_out, levels - 1, steps - 1)
+                    forward(1 - way_out, j - 1, p - lag + steps)
 
     if experts > 1:
         others = mom_in.at[pl.ds(0, experts - 1)]

time: 58.4 us -> 58.3 us (level)
  no operation moved by 1% of the time
where the time goes in v6:
time: 58.3 us; the launch traced here: 57.9 us
  Pallas kernels  56.6 us (97%)
  between operations  1.29 us (2%)
    pallas_call x1, Pallas kernels, body(): pl.pallas_call(functools.partial(kernel, levels, experts, per_holder, cut...  55 us
    pallas_call x1, Pallas kernels, body(): pl.pallas_call(functools.partial(write, WRITES if rows % (8 * WRITES) ==...  1.6 us

profile of v6, /device:TPU:0, one launch (start us, length us, event | category | flops | bytes accessed | tf_op | source)
XLA Modules:
  0.0 57.9 jit_solution(12065312489354206916)
XLA Ops:
  1.3 55.0 %shard_map.163 = (f32[3,768,256]{2,1,0:T(8,128)S(1)}, f32[4,8,6144]{2,1,0:T(8,128)S(1)}) custom-call(bf16[4,2,768,256]{3,2,1,0:T(8,128)(2,1)} %bitcast.8, f32[8,6144]{1,0:T(8,128)} %bitcast.9, f32[8,6144]{1,0:T(8,128)} %bitcast.10, f32[768,256]{1,0:T(8,128)} %w_hbm.1, f32[768,256]{1,0:T(8,128)} %m_hbm.1, f32[768,256]{1,0:T(8,128)} %v_hbm.1, ...), custom_call_target="tpu_custom_call" | custom-call | tf_op jit(solution)/shard_map/pallas_call | solution.py:550
  56.3 1.6 %shard_map.164 = (f32[768,256]{1,0:T(8,128)}, f32[768,256]{1,0:T(8,128)}, f32[768,256]{1,0:T(8,128)}, f32[8,6144]{1,0:T(8,128)}, f32[8,6144]{1,0:T(8,128)}, /*index=5*/f32[8,6144]{1,0:T(8,128)}) custom-call(f32[3,768,256]{2,1,0:T(8,128)S(1)} %get-tuple-element.14.wmv, f32[4,8,6144]{2,1,0:T(8,128)S(1)} %get-tuple-element.15.blocks), custom_call_target="tpu_custom_call" | custom-call | tf_op jit(solution)/shard_map/pallas_call | solution.py:577
